TPU v7x, 32 devices: a whole 2x2x4 slice. The times are simulated.
32 devices in a mesh: ep: 8 (over z, y), dp: 4 (over x, core).
Axes of the slice: x: 2, y: 2, z: 4, core: 2. Of those that a mesh axis runs over, the one named last changes fastest.
Arguments:
- tokens: bfloat16 [6144, 2880], P(('ep', 'dp')), may hold values from -64 to 64
- out_grad: bfloat16 [6144, 2880], P(('ep', 'dp')), may hold values from -6 to 6
- indices: int32 [6144, 4], P(('ep', 'dp')), may hold values from 0 to 31, as said below
- expert_rows: bfloat16 [4, 32, 8, 36, 2880], P('dp', 'ep'), may hold values from -0.111328125 to 0.111328125
- router_weight: bfloat16 [2880, 32], replicated, may hold values from -1 to 1
- router_bias: float32 [32], replicated, may hold values from -3 to 3
- balance_scale: float32 [1], replicated, may hold values from 64 to 256
Outputs:
- token_grad: bfloat16 [6144, 2880], P(('ep', 'dp'))
- weight_grad: float32 [2880, 32], P('dp', 'ep')
- balance_loss: float32 [1], replicated
Inputs may be any that keep to these rules, and one draw needn't show every extreme that they name: `indices`: each row names 4 different experts. Within the 192 rows of one device no expert is named by more than 36 rows, and some expert is named by exactly 36 rows. Within the rows of one device the 4 experts of one ep index (experts j * 4 to j * 4 + 3) are named by at most 108 rows together, and those of some ep index by exactly 108. Every expert is named by some row of every device.
All inputs are finite; a program needn't handle non-finite values.
Results may differ from a plain program's by a relative error of at most 0.0014.
The roundings to bfloat16 on the way count: a program that leaves them out, or rounds other values in their place, can miss the bound.
Values may be sent and summed in bfloat16 or wider, within the bound.
No kernel may reach another device: no remote copies, remote signals or barrier semaphores. Data moves between devices by JAX's collectives and lax.ppermute only.
A program may use at most 128 MiB of HBM per device.

v0:
```python
import math
import jax
import jax.numpy as jnp
from jax import lax
from jax.sharding import PartitionSpec as P


def on_device(tokens, out_grad, indices, expert_rows, router_weight, router_bias, balance_scale):
    tok_dev = tokens.shape[0]
    chosen = indices.shape[1]
    width = tokens.shape[1]
    experts = router_weight.shape[1]
    capacity = expert_rows.shape[3]
    ep_size = lax.axis_size("ep")
    dp_size = lax.axis_size("dp")
    token_total = tok_dev * ep_size * dp_size
    expert_ids = jnp.arange(experts, dtype=jnp.int32)
    onehot = (indices[:, :, None] == expert_ids[None, None, :]).astype(jnp.float32)
    named_by = jnp.sum(onehot, axis=1)
    local_counts = jnp.sum(named_by, axis=0)
    logits = jnp.dot(tokens, router_weight, preferred_element_type=jnp.float32) + router_bias
    probability = jax.nn.softmax(logits, axis=-1)
    counts, prob_sums = lax.psum((local_counts, jnp.sum(probability, axis=0)), ("ep", "dp"))
    share_of = counts / (token_total * chosen)
    balance_loss = (experts * jnp.sum(share_of * (prob_sums / token_total))).reshape(1)
    row_ids = jnp.arange(tok_dev, dtype=jnp.int32)
    lower_mask = (row_ids[:, None] > row_ids[None, :]).astype(jnp.bfloat16)
    before = jnp.dot(lower_mask, named_by.astype(jnp.bfloat16), preferred_element_type=jnp.float32)
    slot_index = jnp.sum(onehot * before[:, None, :], axis=2).astype(jnp.int32)
    returned = lax.all_to_all(expert_rows, "ep", split_axis=2, concat_axis=1, tiled=True)
    flat_rows = returned.reshape(experts * capacity, width)
    row_index = indices * capacity + slot_index
    picked = jnp.take(flat_rows, row_index, axis=0)
    pair_dots = jnp.einsum("td,tkd->tk", out_grad, picked, preferred_element_type=jnp.float32)
    chosen_logits = jnp.take_along_axis(logits, indices, axis=1)
    mix_weight = jax.nn.softmax(chosen_logits, axis=-1)
    sel_grad = mix_weight * (pair_dots - jnp.sum(mix_weight * pair_dots, axis=1, keepdims=True))
    balance_push = balance_scale[0] * experts * share_of
    spread = probability * (
        balance_push[None, :] - jnp.sum(probability * balance_push[None, :], axis=1, keepdims=True)
    )
    logit_grad = (spread + jnp.sum(onehot * sel_grad[:, :, None], axis=1)).astype(jnp.bfloat16)
    token_grad = lax.dot_general(
        logit_grad, router_weight, (((1,), (1,)), ((), ())), preferred_element_type=jnp.float32
    ).astype(jnp.bfloat16)
    term = lax.dot_general(
        tokens, logit_grad, (((0,), (0,)), ((), ())), preferred_element_type=jnp.float32
    )
    summed = lax.psum_scatter(term, "ep", scatter_dimension=1, tiled=True)
    summed = lax.psum_scatter(summed, "dp", scatter_dimension=0, tiled=True)
    weight_grad = summed / math.sqrt(token_total)
    return (token_grad, weight_grad, balance_loss)


def solution(mesh):
    placed = (
        P(("ep", "dp"), None),
        P(("ep", "dp"), None),
        P(("ep", "dp"), None),
        P("dp", "ep", None, None, None),
        P(),
        P(),
        P(),
    )
    return jax.shard_map(
        on_device,
        mesh=mesh,
        in_specs=placed,
        out_specs=(P(("ep", "dp"), None), P("dp", "ep"), P()),
        check_vma=False,
    )
```

profile of v0, /device:TPU:0, one launch (start us, length us, event | category | flops | bytes accessed | tf_op | source)
XLA Modules:
  0.0 366.3 jit_solution(14106931418418347998)
XLA Ops:
  7.2 7.0 %copy.48 = bf16[1,4,8,36,2880]{4,3,1,0,2:T(8,128)(2,1)} copy(bf16[1,4,8,36,2880]{4,2,3,1,0:T(8,128)(2,1)} %param.10) | data formatting | bytes 13271040 | tf_op args[3]
  14.2 7.5 %all-to-all-start = ((bf16[1,4,8,36,2880]{4,3,1,0,2:T(8,128)(2,1)}), bf16[1,4,8,36,2880]{4,3,1,0,2:T(8,128)(2,1)}, u32[]{:S(2)}, u32[]{:S(2)}) async-start(bf16[1,4,8,36,2880]{4,3,1,0,2:T(8,128)(2,1)} %copy.48), calls=%async_computation | async-start | bytes 15073280 | tf_op jit(solution)/shard_map/all_to_all | solution.py:30
  21.8 0.1 fusion.5
  21.9 0.2 convert_reduce_fusion.1
  22.1 184.7 %psum.14 = f32[32]{0:T(128)S(1)} all-reduce(f32[32]{0:T(128)S(1)} %get-tuple-element.5), channel_id=1, replica_groups=mesh['ep'=8,'dp'=4] {'ep','dp'}, use_global_device_ids=true, to_apply=%region_3.0 | all-reduce | flops 32 | bytes 256 | tf_op jit(solution)/shard_map/psum | solution.py:23
  207.0 0.2 copy.47
  207.4 0.5 fusion.16
  207.9 6.3 %gather_fusion.1 = f32[768]{0:T(1024)S(1)} fusion(f32[192,32]{0,1:T(8,128)S(1)} %get-tuple-element.12, s32[768]{0:T(1024)S(1)} %reshape.51), kind=kCustom, calls=%fused_computation.1 | custom fusion | bytes 12288 | tf_op jit(solution)/shard_map/jit(take_along_axis)/gather | solution.py:35
  215.2 0.1 fusion.14
  215.4 9.3 %reshape.41 = bf16[1152,2880]{1,0:T(8,128)(2,1)} reshape(bf16[1,8,4,1,36,2880]{5,4,2,1,3,0:T(8,128)(2,1)} %bitcast.3) | data formatting | bytes 13271040 | tf_op jit(solution)/shard_map/reshape | solution.py:31
  224.7 13.1 %gather_fusion = bf16[768,2880]{1,0:T(8,128)(2,1)} fusion(bf16[1152,2880]{1,0:T(8,128)(2,1)} %reshape.41, s32[1024]{0:T(1024)S(1)} %pad_clamp_fusion), kind=kCustom, calls=%fused_computation | custom fusion | bytes 8850432 | tf_op jit(solution)/shard_map/jit(_take)/gather | solution.py:33
  237.8 7.1 %reshape.44 = bf16[192,4,2880]{2,1,0:T(4,128)(2,1)} reshape(bf16[768,2880]{1,0:T(8,128)(2,1)} %gather_fusion) | data formatting | bytes 8847360 | tf_op jit(solution)/shard_map/jit(_take)/gather | solution.py:33
  244.9 9.4 %fusion = f32[192,1,4]{2,1,0:T(1,128)S(1)} fusion(bf16[192,4,2880]{2,1,0:T(4,128)(2,1)} %reshape.44, pred[192,4]{1,0:T(8,128)(4,1)S(1)} %copy.47, bf16[192,2880,1]{1,0,2:T(8,128)(2,1)S(1)} %bitcast.30), kind=kOutput, calls=%fused_computation.2 | convolution fusion | flops 6635520 | bytes 5533440 | tf_op jit(solution)/shard_map/td,tkd->tk/dot_general | solution.py:34
  254.6 1.1 convolution_bitcast_fusion
  255.7 39.3 %psum.15 = f32[32]{0:T(128)S(1)} all-reduce(f32[32]{0:T(128)S(1)} %get-tuple-element.3), channel_id=1, replica_groups=mesh['ep'=8,'dp'=4] {'ep','dp'}, use_global_device_ids=true, to_apply=%region_14.15 | all-reduce | flops 32 | bytes 256 | tf_op jit(solution)/shard_map/psum | solution.py:23
  295.0 0.6 dynamic-slice
  296.3 0.6 multiply_reduce_fusion.1
  297.5 29.8 %all-reduce.3.cloned.1.call-done = f32[2880,32]{0,1:T(8,128)} async-done(((f32[2880,32]{0,1:T(8,128)}), f32[2880,32]{0,1:T(8,128)}) %all-reduce.3.cloned.1.call-update) | async-done | bytes 368656
  327.3 0.9 constant_dynamic-slice_fusion
  328.2 1.6 copy.52
  329.9 1.5 convolution_convert_fusion
  331.4 25.2 %reduce-scatter.4.cloned.1.call-done = f32[720,4]{1,0:T(8,128)} async-done(((f32[2880,4]{1,0:T(8,128)}), f32[720,4]{1,0:T(8,128)}) %reduce-scatter.4.cloned.1.call-update) | async-done | bytes 11536
  356.6 1.1 copy.53
  357.7 0.6 broadcast_multiply_fusion
  (36 shorter events, 1.2 us)
Async XLA Ops:
  7.2 237.8 %copy-start = (bf16[192,2880]{1,0:T(8,128)(2,1)S(1)}, bf16[192,2880]{1,0:T(8,128)(2,1)}, u32[]{:S(2)}) copy-start(bf16[192,2880]{1,0:T(8,128)(2,1)} %param.8) | copy-start | bytes 3317764
  14.2 7.5 %copy-start.3 = (s32[192,4]{0,1:T(4,128)S(1)}, s32[192,4]{0,1:T(4,128)}, u32[]{:S(2)}) copy-start(s32[192,4]{0,1:T(4,128)} %param.9) | copy-start | bytes 9220
  14.2 193.2 %copy-start.1 = (bf16[192,2880]{1,0:T(8,128)(2,1)S(1)}, bf16[192,2880]{1,0:T(8,128)(2,1)}, u32[]{:S(2)}) copy-start(bf16[192,2880]{1,0:T(8,128)(2,1)} %param.7) | copy-start | bytes 3317764
  14.2 193.2 %copy-start.2 = (bf16[2880,32]{0,1:T(8,128)(2,1)S(1)}, bf16[2880,32]{0,1:T(8,128)(2,1)}, u32[]{:S(2)}) copy-start(bf16[2880,32]{0,1:T(8,128)(2,1)} %param.11) | copy-start | bytes 552964
  14.2 193.2 %copy-start.4 = (f32[32]{0:T(128)S(1)}, f32[32]{0:T(128)}, u32[]{:S(2)}) copy-start(f32[32]{0:T(128)} %param.12) | copy-start | bytes 388
  14.2 201.1 %all-to-all-start = ((bf16[1,4,8,36,2880]{4,3,1,0,2:T(8,128)(2,1)}), bf16[1,4,8,36,2880]{4,3,1,0,2:T(8,128)(2,1)}, u32[]{:S(2)}, u32[]{:S(2)}) async-start(bf16[1,4,8,36,2880]{4,3,1,0,2:T(8,128)(2,1)} %copy.48), calls=%async_computation | async-start | bytes 15073280 | tf_op jit(solution)/shard_map/all_to_all | solution.py:30
  21.7 305.6 %all-reduce.3.cloned.1.call-start = ((), (), s32[]{:S(2)}) async-start(), calls=%async_computation.3 | async-start | bytes 753664
  244.9 50.1 %copy-start.5 = (u32[32]{0:T(128)S(1)}, u32[32]{0:T(128)}, u32[]{:S(2)}) copy-start(u32[32]{0:T(128)} %constant.70) | copy-start | bytes 388
  255.7 100.9 %reduce-scatter.4.cloned.1.call-start = ((), (), s32[]{:S(2)}) async-start(), calls=%async_computation.2 | async-start | bytes 1843200
Sparse Core Ops, SparseCore 0:
  255.8 71.4 all-reduce.2
  330.0 26.5 reduce-scatter.3
where the time goes:
time: 367 us; the launch traced here: 366 us
  blocking collectives  224 us (61%)
  waiting for transfers between devices  55.1 us (15%)
  local copies, waits for them, and re-layouts  48.1 us (13%)
  between operations  17.3 us (5%)
  matrix products  12.6 us (3%)
  starting transfers between devices  7.53 us (2%)
    psum x2, blocking collectives, on_device(): lax.psum((local_counts, jnp.sum(probability, axis=0)), ('ep', 'dp'))  224 us
    unnamed x4, waiting for transfers between devices  55.1 us
    gather x2, local copies, waits for them, and re-layouts, on_device(): picked = jnp.take(flat_rows, row_index, axis=0)  20.2 us
    unnamed x17, local copies, waits for them, and re-layouts  11.3 us
    dot_general x1, matrix products, on_device(): jnp.einsum('td,tkd->tk', out_grad, picked, preferred_element_type=jnp.flo...  9.4 us
    reshape x1, local copies, waits for them, and re-layouts, on_device(): flat_rows = returned.reshape(experts * capacity, width)  9.32 us
    all_to_all x1, starting transfers between devices, on_device(): lax.all_to_all(expert_rows, 'ep', split_axis=2, concat_axis=1, tiled=True)  7.45 us
  transfers between devices with their start and end apart: 3, of which 2 were waited for; matrix products, arithmetic and copies ran while one was open for 3% of the time, Pallas kernels for 0%

commit v1 on v0

--- a/solution.py
+++ b/solution.py
@@ -20,7 +20,8 @@
     local_counts = jnp.sum(named_by, axis=0)
     logits = jnp.dot(tokens, router_weight, preferred_element_type=jnp.float32) + router_bias
     probability = jax.nn.softmax(logits, axis=-1)
-    counts, prob_sums = lax.psum((local_counts, jnp.sum(probability, axis=0)), ("ep", "dp"))
+    _match_vector = lambda t0: jax.lax.psum(jax.lax.psum(t0, axis_name="ep"), axis_name="dp")
+    counts, prob_sums = _match_vector((local_counts, jnp.sum(probability, axis=0)))
     share_of = counts / (token_total * chosen)
     balance_loss = (experts * jnp.sum(share_of * (prob_sums / token_total))).reshape(1)
     row_ids = jnp.arange(tok_dev, dtype=jnp.int32)

time: 367 us -> 352 us (0.959)
  blocking collectives: 224 us -> 185 us
  waiting for transfers between devices: 55.1 us -> 78.8 us
    psum x2 -> x4, blocking collectives: 224 us -> 185 us  [the longest x2 173 us: on_device(): jax.lax.psum(t0, axis_name='ep')]
    unnamed x4, waiting for transfers between devices: 55.1 us -> 68 us
    all_to_all x1, waiting for transfers between devices: 0.01 us -> 10.8 us  [on_device(): lax.all_to_all(expert_rows, 'ep', split_axis=2, concat_axis=1, tiled=True)]
  transfers between devices with their start and end apart: 3 -> 3, of which waited for: 2 -> 3; matrix products, arithmetic and copies ran while one was open for 3% -> 3% of each run, Pallas kernels for 0% -> 0%
where the time goes in v1:
time: 352 us; the launch traced here: 351 us
  blocking collectives  185 us (53%)
  waiting for transfers between devices  78.8 us (22%)
  local copies, waits for them, and re-layouts  48.1 us (14%)
  between operations  17.3 us (5%)
  matrix products  12.6 us (4%)
  starting transfers between devices  7.53 us (2%)
    psum x2, blocking collectives, on_device(): jax.lax.psum(t0, axis_name='ep')  173 us
    unnamed x4, waiting for transfers between devices  68 us
    gather x2, local copies, waits for them, and re-layouts, on_device(): picked = jnp.take(flat_rows, row_index, axis=0)  20.2 us
    psum x2, blocking collectives, on_device(): jax.lax.psum(jax.lax.psum(t0, axis_name='ep'), axis_name='dp')  12.1 us
    unnamed x17, local copies, waits for them, and re-layouts  11.3 us
    all_to_all x1, waiting for transfers between devices, on_device(): lax.all_to_all(expert_rows, 'ep', split_axis=2, concat_axis=1, tiled=True)  10.8 us
    dot_general x1, matrix products, on_device(): jnp.einsum('td,tkd->tk', out_grad, picked, preferred_element_type=jnp.flo...  9.4 us
    reshape x1, local copies, waits for them, and re-layouts, on_device(): flat_rows = returned.reshape(experts * capacity, width)  9.31 us
  transfers between devices with their start and end apart: 3, of which 3 were waited for; matrix products, arithmetic and copies ran while one was open for 3% of the time, Pallas kernels for 0%

profile of v1, /device:TPU:0, one launch (start us, length us, event | category | flops | bytes accessed | tf_op | source)
XLA Modules:
  0.0 351.1 jit_solution(17235843222115780855)
XLA Ops:
  7.2 7.0 %copy.48 = bf16[1,4,8,36,2880]{4,3,1,0,2:T(8,128)(2,1)} copy(bf16[1,4,8,36,2880]{4,2,3,1,0:T(8,128)(2,1)} %param.10) | data formatting | bytes 13271040 | tf_op args[3]
  14.2 7.5 %all-to-all-start = ((bf16[1,4,8,36,2880]{4,3,1,0,2:T(8,128)(2,1)}), bf16[1,4,8,36,2880]{4,3,1,0,2:T(8,128)(2,1)}, u32[]{:S(2)}, u32[]{:S(2)}) async-start(bf16[1,4,8,36,2880]{4,3,1,0,2:T(8,128)(2,1)} %copy.48), calls=%async_computation | async-start | bytes 15073280 | tf_op jit(solution)/shard_map/all_to_all | solution.py:31
  21.9 0.2 convert_reduce_fusion.1
  22.8 0.5 fusion.16
  23.3 6.3 %gather_fusion.1 = f32[768]{0:T(1024)S(1)} fusion(f32[192,32]{0,1:T(8,128)S(1)} %get-tuple-element.12, s32[768]{0:T(1024)S(1)} %reshape.51), kind=kCustom, calls=%fused_computation.1 | custom fusion | bytes 12288 | tf_op jit(solution)/shard_map/jit(take_along_axis)/gather | solution.py:36
  30.5 139.1 %psum.28 = f32[32]{0:T(128)S(1)} all-reduce(f32[32]{0:T(128)S(1)} %get-tuple-element.5), channel_id=1, replica_groups=mesh['ep'=8,'dp'=4] {'ep'}, use_global_device_ids=true, to_apply=%region_3.0 | all-reduce | flops 32 | bytes 256 | tf_op jit(solution)/shard_map/psum | solution.py:23
  169.6 6.0 %psum.29 = f32[32]{0:T(128)S(1)} all-reduce(f32[32]{0:T(128)S(1)} %psum.28), channel_id=1, replica_groups=mesh['ep'=8,'dp'=4] {'dp'}, use_global_device_ids=true, to_apply=%region_4.0 | all-reduce | flops 32 | bytes 256 | tf_op jit(solution)/shard_map/psum | solution.py:23
  175.9 10.8 %all-to-all-done = bf16[1,4,8,36,2880]{4,3,1,0,2:T(8,128)(2,1)} async-done(((bf16[1,4,8,36,2880]{4,3,1,0,2:T(8,128)(2,1)}), bf16[1,4,8,36,2880]{4,3,1,0,2:T(8,128)(2,1)}, u32[]{:S(2)}, u32[]{:S(2)}) %all-to-all-start) | async-done | bytes 6635552 | tf_op jit(solution)/shard_map/all_to_all | solution.py:31
  186.7 9.3 %reshape.41 = bf16[1152,2880]{1,0:T(8,128)(2,1)} reshape(bf16[1,8,4,1,36,2880]{5,4,2,1,3,0:T(8,128)(2,1)} %bitcast.3) | data formatting | bytes 13271040 | tf_op jit(solution)/shard_map/reshape | solution.py:32
  196.0 13.1 %gather_fusion = bf16[768,2880]{1,0:T(8,128)(2,1)} fusion(bf16[1152,2880]{1,0:T(8,128)(2,1)} %reshape.41, s32[1024]{0:T(1024)S(1)} %pad_clamp_fusion), kind=kCustom, calls=%fused_computation | custom fusion | bytes 8850432 | tf_op jit(solution)/shard_map/jit(_take)/gather | solution.py:34
  209.1 7.1 %reshape.44 = bf16[192,4,2880]{2,1,0:T(4,128)(2,1)} reshape(bf16[768,2880]{1,0:T(8,128)(2,1)} %gather_fusion) | data formatting | bytes 8847360 | tf_op jit(solution)/shard_map/jit(_take)/gather | solution.py:34
  216.2 9.4 %fusion = f32[192,1,4]{2,1,0:T(1,128)S(1)} fusion(bf16[192,4,2880]{2,1,0:T(4,128)(2,1)} %reshape.44, pred[192,4]{1,0:T(8,128)(4,1)S(1)} %copy.47, bf16[192,2880,1]{1,0,2:T(8,128)(2,1)S(1)} %bitcast.30), kind=kOutput, calls=%fused_computation.2 | convolution fusion | flops 6635520 | bytes 5533440 | tf_op jit(solution)/shard_map/td,tkd->tk/dot_general | solution.py:35
  225.9 1.1 convolution_bitcast_fusion
  227.1 0.6 dynamic-slice
  228.3 33.8 %psum.30 = f32[32]{0:T(128)S(1)} all-reduce(f32[32]{0:T(128)S(1)} %get-tuple-element.3), channel_id=1, replica_groups=mesh['ep'=8,'dp'=4] {'ep'}, use_global_device_ids=true, to_apply=%region_15.16 | all-reduce | flops 32 | bytes 256 | tf_op jit(solution)/shard_map/psum | solution.py:23
  262.1 6.0 %psum.31 = f32[32]{0:T(128)S(1)} all-reduce(f32[32]{0:T(128)S(1)} %psum.30), channel_id=1, replica_groups=mesh['ep'=8,'dp'=4] {'dp'}, use_global_device_ids=true, to_apply=%region_16.17 | all-reduce | flops 32 | bytes 256 | tf_op jit(solution)/shard_map/psum | solution.py:23
  268.1 0.6 multiply_reduce_fusion.1
  269.4 42.7 %all-reduce.3.cloned.1.call-done = f32[2880,32]{0,1:T(8,128)} async-done(((f32[2880,32]{0,1:T(8,128)}), f32[2880,32]{0,1:T(8,128)}) %all-reduce.3.cloned.1.call-update) | async-done | bytes 368656
  312.1 0.9 constant_dynamic-slice_fusion
  313.0 1.6 copy.52
  314.6 1.5 convolution_convert_fusion
  316.1 25.2 %reduce-scatter.4.cloned.1.call-done = f32[720,4]{1,0:T(8,128)} async-done(((f32[2880,4]{1,0:T(8,128)}), f32[720,4]{1,0:T(8,128)}) %reduce-scatter.4.cloned.1.call-update) | async-done | bytes 11536
  341.4 1.1 copy.53
  342.5 0.6 broadcast_multiply_fusion
  (38 shorter events, 1.6 us)
Async XLA Ops:
  7.2 209.1 %copy-start = (bf16[192,2880]{1,0:T(8,128)(2,1)S(1)}, bf16[192,2880]{1,0:T(8,128)(2,1)}, u32[]{:S(2)}) copy-start(bf16[192,2880]{1,0:T(8,128)(2,1)} %param.8) | copy-start | bytes 3317764
  14.2 7.5 %copy-start.3 = (s32[192,4]{0,1:T(4,128)S(1)}, s32[192,4]{0,1:T(4,128)}, u32[]{:S(2)}) copy-start(s32[192,4]{0,1:T(4,128)} %param.9) | copy-start | bytes 9220
  14.2 8.5 %copy-start.1 = (bf16[192,2880]{1,0:T(8,128)(2,1)S(1)}, bf16[192,2880]{1,0:T(8,128)(2,1)}, u32[]{:S(2)}) copy-start(bf16[192,2880]{1,0:T(8,128)(2,1)} %param.7) | copy-start | bytes 3317764
  14.2 8.5 %copy-start.2 = (bf16[2880,32]{0,1:T(8,128)(2,1)S(1)}, bf16[2880,32]{0,1:T(8,128)(2,1)}, u32[]{:S(2)}) copy-start(bf16[2880,32]{0,1:T(8,128)(2,1)} %param.11) | copy-start | bytes 552964
  14.2 8.5 %copy-start.4 = (f32[32]{0:T(128)S(1)}, f32[32]{0:T(128)}, u32[]{:S(2)}) copy-start(f32[32]{0:T(128)} %param.12) | copy-start | bytes 388
  14.2 172.5 %all-to-all-start = ((bf16[1,4,8,36,2880]{4,3,1,0,2:T(8,128)(2,1)}), bf16[1,4,8,36,2880]{4,3,1,0,2:T(8,128)(2,1)}, u32[]{:S(2)}, u32[]{:S(2)}) async-start(bf16[1,4,8,36,2880]{4,3,1,0,2:T(8,128)(2,1)} %copy.48), calls=%async_computation | async-start | bytes 15073280 | tf_op jit(solution)/shard_map/all_to_all | solution.py:31
  21.7 290.4 %all-reduce.3.cloned.1.call-start = ((), (), s32[]{:S(2)}) async-start(), calls=%async_computation.3 | async-start | bytes 753664
  216.2 10.8 %copy-start.5 = (u32[32]{0:T(128)S(1)}, u32[32]{0:T(128)}, u32[]{:S(2)}) copy-start(u32[32]{0:T(128)} %constant.70) | copy-start | bytes 388
  227.0 114.4 %reduce-scatter.4.cloned.1.call-start = ((), (), s32[]{:S(2)}) async-start(), calls=%async_computation.2 | async-start | bytes 1843200
Sparse Core Ops, SparseCore 0:
  227.1 84.9 all-reduce.2
  314.8 26.5 reduce-scatter.3
